TPU v7x, 32 devices: a whole 2x2x4 slice. The times are simulated.
32 devices in a mesh: seq: 8 (over z, x), head: 4 (over y, core).
Axes of the slice: x: 2, y: 2, z: 4, core: 2. Of those that a mesh axis runs over, the one named last changes fastest.
Arguments:
- tokens: bfloat16 [2048, 4608], P('seq', 'head'), may hold values from -32 to 32
- segments: int32 [2048], P('seq'), may hold values from 0 to 7, never falling along the last dimension, each value on 1 to 1024 neighbouring positions
- pre_gain: float32 [4608], replicated, may hold values from 0.1 to 1.9
- post_gain: float32 [4608], replicated, may hold values from 0.1 to 1.9
- w_query: bfloat16 [4608, 1024], P('seq', 'head'), may hold values from -0.375 to 0.375
- w_key: bfloat16 [4608, 512], P('seq', 'head'), may hold values from -0.1875 to 0.1875
- w_value: bfloat16 [4608, 512], P('seq', 'head'), may hold values from -0.09375 to 0.09375
- w_out: bfloat16 [1024, 4608], P('head', 'seq'), may hold values from -0.1875 to 0.1875
Outputs:
- mixed: bfloat16 [2048, 4608], P('seq')
Inputs may be any that keep to these rules, and one draw needn't show every extreme that they name: `segments`: segment ids never fall; each of the 8 documents holds at least one token and at most 1024, one exactly 1024.
All inputs are finite; a program needn't handle non-finite values.
Results may differ from a plain program's by a relative error of at most 0.01.
Values may be sent and summed in bfloat16 or wider, within the bound.
A program may use at most 64 MiB of HBM per device.

v0:
```python
import jax
import jax.numpy as jnp
from jax import lax
from jax.sharding import PartitionSpec as P

HD = 128
GROUP = 2
SCALAR = 144
DOCS = 8
EPS = 1e-06
CAP = 50.0


def carried_in(value, axis, join, neutral):
    count, mine = (lax.axis_size(axis), lax.axis_index(axis))
    pieces = lax.all_gather(value, axis)
    subtotal = jnp.full_like(value, 0) + jnp.asarray(neutral, value.dtype)

    def step(position, subtotal):
        longer = join(subtotal, pieces[position])
        return jnp.where(position < mine, longer, subtotal)

    return lax.fori_loop(0, count - 1, step, subtotal)


def rotate(values, position, width):
    count = values.shape[1] // width
    half = width // 2
    shaped = values.reshape(values.shape[0], count, width)
    freq = 10000.0 ** (-(jnp.arange(half, dtype=jnp.float32) / half))
    angle = position[:, None] * freq[None, :]
    cosine = jnp.cos(angle)[:, None, :]
    sine = jnp.sin(angle)[:, None, :]
    first = shaped[:, :, :half]
    second = shaped[:, :, half:]
    turned = jnp.concatenate(
        [first * cosine - second * sine, second * cosine + first * sine], axis=2
    )
    return turned.reshape(values.shape[0], count * width)


def add_counts(earlier, later):
    return earlier + later


def local(tokens, segments, pre_gain, post_gain, w_query, w_key, w_value, w_out):
    rows = tokens.shape[0]
    whole = lax.all_gather(tokens, "head", axis=1, tiled=True)
    wide = whole.astype(jnp.float32)
    normed = (
        wide * lax.rsqrt(jnp.mean(wide * wide, axis=1, keepdims=True) + EPS) * pre_gain
    ).astype(jnp.bfloat16)
    pieces = (
        lax.all_gather(w_query, "seq", axis=0, tiled=True),
        lax.all_gather(w_key, "seq", axis=0, tiled=True),
        lax.all_gather(w_value, "seq", axis=0, tiled=True),
    )
    query, key_proj, value_proj = tuple(
        (jnp.dot(normed, piece, preferred_element_type=jnp.float32) for piece in pieces)
    )
    levels = jnp.arange(DOCS, dtype=jnp.int32)
    below = jnp.sum((levels[None, :] > segments[:, None]).astype(jnp.float32), axis=0)
    earlier = carried_in(below, "seq", add_counts, jnp.zeros((DOCS,), jnp.float32))
    starts = earlier + below
    onehot = (segments[:, None] == levels[None, :]).astype(jnp.float32)
    tok_start = jnp.sum(onehot * starts[None, :], axis=1)
    offset = lax.axis_index("seq") * rows
    index_f = (offset + jnp.arange(rows, dtype=jnp.int32)).astype(jnp.float32)
    position = index_f - tok_start
    kv_count = w_key.shape[1] // HD
    rq = (rotate(query, position, HD) * SCALAR ** (-0.5)).astype(jnp.bfloat16)
    rk = rotate(key_proj, position, HD).astype(jnp.bfloat16)
    vb = value_proj.astype(jnp.bfloat16)
    stacked = (
        rq.reshape(rows, kv_count, GROUP, HD)
        .transpose(1, 2, 0, 3)
        .reshape(kv_count, GROUP * rows, HD)
    )
    query_start = jnp.tile(tok_start, GROUP)
    query_index = jnp.tile(index_f, GROUP)
    empty = (
        jnp.zeros((kv_count, GROUP * rows, HD), jnp.float32),
        jnp.zeros((kv_count, GROUP * rows), jnp.float32),
    )
    keys_all = lax.all_gather(rk, "seq", axis=0, tiled=True)
    values_all = lax.all_gather(vb, "seq", axis=0, tiled=True)
    count = keys_all.shape[0]
    block = 1024
    steps_total = count // block

    def compute(offset_blk, state):
        numer, denom = state
        keys_blk = lax.dynamic_slice_in_dim(keys_all, offset_blk, block, 0).reshape(
            block, kv_count, HD
        )
        values_blk = lax.dynamic_slice_in_dim(values_all, offset_blk, block, 0).reshape(
            block, kv_count, HD
        )
        key_index = (offset_blk + jnp.arange(block, dtype=jnp.int32)).astype(jnp.float32)
        scores = jnp.einsum("cqd,kcd->cqk", stacked, keys_blk, preferred_element_type=jnp.float32)
        capped = CAP * jnp.tanh(scores / CAP)
        allowed = (key_index[None, None, :] >= query_start[None, :, None]) & (
            key_index[None, None, :] <= query_index[None, :, None]
        )
        weights = jnp.where(allowed, jnp.exp(capped), 0.0)
        numer = numer + jnp.einsum(
            "cqk,kcd->cqd",
            weights.astype(jnp.bfloat16),
            values_blk,
            preferred_element_type=jnp.float32,
        )
        denom = denom + jnp.sum(weights, axis=2)
        return (numer, denom)

    def one_block(step, state):
        offset_blk = step * block
        return compute(offset_blk, state)

    numer, denom = lax.fori_loop(0, steps_total, one_block, empty)
    attn = (numer / denom[:, :, None]).reshape(kv_count, GROUP, rows, HD).transpose(2, 0, 1, 3)
    attn = attn.reshape(rows, kv_count * GROUP * HD).astype(jnp.bfloat16)
    partial_proj = jnp.dot(
        attn, lax.all_gather(w_out, "seq", axis=1, tiled=True), preferred_element_type=jnp.float32
    )
    partial_proj = lax.optimization_barrier(partial_proj.astype(jnp.bfloat16)).astype(jnp.float32)
    summed = lax.psum(partial_proj.astype(jnp.bfloat16), "head").astype(jnp.float32)
    scale = lax.rsqrt(jnp.mean(summed * summed, axis=1, keepdims=True) + EPS)
    return (wide + summed * scale * post_gain).astype(jnp.bfloat16)


def solution(mesh):
    return jax.shard_map(
        local,
        mesh=mesh,
        in_specs=(
            P("seq", "head"),
            P("seq"),
            P(),
            P(),
            P("seq", "head"),
            P("seq", "head"),
            P("seq", "head"),
            P("head", "seq"),
        ),
        out_specs=P("seq", None),
        check_vma=False,
    )
```

profile of v0, /device:TPU:0, one launch (start us, length us, event | category | flops | bytes accessed | tf_op | source)
XLA Modules:
  0.0 300.0 jit_solution(1061354986700771852)
XLA Ops:
  6.5 0.7 all-gather.8.cloned.1.call-update
  7.3 0.7 all-gather.10.cloned.1.call-update
  8.1 0.7 all-gather.14.cloned.1.call-update
  10.0 0.8 convert_reduce_fusion
  10.8 1.3 dynamic-slice
  12.9 23.1 %all-reduce = f32[64]{0:T(128)S(1)} all-reduce(f32[64]{0:T(128)S(1)} %dynamic-update-slice), channel_id=2, replica_groups=mesh['seq'=8,'head'=4] {'seq'}, use_global_device_ids=true, to_apply=%add | all-reduce | flops 64 | bytes 512
  36.4 0.8 select_reduce_fusion
  37.5 2.4 fusion.14
  39.9 39.1 %all-gather.10.cloned.1.call-done = bf16[4608,128]{1,0:T(8,128)(2,1)} async-done(((bf16[576,128]{1,0:T(8,128)(2,1)}), bf16[4608,128]{1,0:T(8,128)(2,1)}) %all-gather.10.cloned.1.call-update) | async-done | bytes 1179664 | tf_op jit(solution)/shard_map/all_gather | solution.py:55
  79.0 2.3 convolution_bitcast_fusion.1
  81.7 34.4 %all-gather.1 = bf16[2048,1,128]{0,2,1:T(8,128)(2,1)} all-gather(bf16[256,1,128]{0,2,1:T(8,128)(2,1)S(1)} %pad_maximum_fusion), channel_id=3, replica_groups=mesh['seq'=8,'head'=4] {'seq'}, dimensions={0}, use_global_device_ids=true | all-gather | bytes 589824 | tf_op jit(solution)/shard_map/all_gather | solution.py:85
  116.1 6.3 %all-gather.14.cloned.1.call-done = bf16[4608,128]{1,0:T(8,128)(2,1)} async-done(((bf16[576,128]{1,0:T(8,128)(2,1)}), bf16[4608,128]{1,0:T(8,128)(2,1)}) %all-gather.14.cloned.1.call-update) | async-done | bytes 1179664 | tf_op jit(solution)/shard_map/all_gather | solution.py:56
  122.4 2.2 convolution_convert_fusion.1
  124.6 32.3 %all_gather.34 = bf16[2048,128]{1,0:T(8,128)(2,1)S(1)} all-gather(bf16[256,128]{1,0:T(8,128)(2,1)S(1)} %convolution_convert_fusion.1), channel_id=1, replica_groups=mesh['seq'=8,'head'=4] {'seq'}, dimensions={0}, use_global_device_ids=true | all-gather | bytes 589824 | tf_op jit(solution)/shard_map/all_gather | solution.py:86
  156.9 20.0 %all-gather.12.cloned.1.call-done = bf16[4608,256]{1,0:T(8,128)(2,1)} async-done(((bf16[576,256]{1,0:T(8,128)(2,1)}), bf16[4608,256]{1,0:T(8,128)(2,1)}) %all-gather.12.cloned.1.call-update) | async-done | bytes 2359312 | tf_op jit(solution)/shard_map/all_gather | solution.py:54
  177.0 3.0 fusion.30
  180.1 5.0 %while.31 = (s32[]{:T(128)}, f32[1,512,128]{2,1,0:T(8,128)S(1)}, f32[1,512]{1,0:T(1,128)S(1)}, bf16[2048,128]{0,1:T(8,128)(2,1)}, bf16[1,512,128]{2,1,0:T(8,128)...) while((s32[]{:T(128)}, f32[1,512,128]{2,1,0:T(8,128)S(1)}, ...), condition=%wide.region_7.8_spmd.clone, body=%wide.region_5.7_spmd.clone.sunk | while | flops 272763392 | bytes 3311802 | solution.py:119
  180.2 1.9 fusion.47
  182.7 1.9 fusion.47
  185.4 44.5 %all-gather.16.cloned.1.call-done = bf16[256,4608]{0,1:T(8,128)(2,1)} async-done(((bf16[256,576]{0,1:T(8,128)(2,1)}), bf16[256,4608]{0,1:T(8,128)(2,1)}) %all-gather.16.cloned.1.call-update) | async-done | bytes 2359312 | tf_op jit(solution)/shard_map/all_gather | solution.py:123
  229.9 3.9 %convolution_convert_fusion = bf16[256,4608]{1,0:T(8,128)(2,1)} fusion(bf16[256,256]{0,1:T(8,128)(2,1)S(1)} %bitcast.59, bf16[256,4608]{0,1:T(8,128)(2,1)} %all-gather.16.cloned.1.call-done), kind=kOutput, calls=%fused_computation.21 | convolution fusion | flops 605159424 | bytes 4849664 | tf_op jit(solution)/shard_map/dot_general | solution.py:122
  233.9 54.4 %all-reduce.3.cloned.1.call-done = bf16[256,4608]{1,0:T(8,128)(2,1)} async-done(((bf16[256,4608]{1,0:T(8,128)(2,1)}), bf16[256,4608]{1,0:T(8,128)(2,1)}) %all-reduce.3.cloned.1.call-update) | async-done | bytes 2359312 | tf_op jit(solution)/shard_map/psum | solution.py:126
  288.2 2.4 fusion.12
  290.6 2.6 fusion.17
  (60 shorter events, 4.2 us)
Async XLA Ops:
  6.5 72.5 %copy-start.4 = (f32[4608]{0:T(1024)S(1)}, f32[4608]{0:T(1024)}, u32[]{:S(2)}) copy-start(f32[4608]{0:T(1024)} %param.14) | copy-start | bytes 55300
  6.5 31.0 %all-gather.8.cloned.1.call-start = ((), (), s32[]{:S(2)}) async-start(), calls=%async_computation | async-start | bytes 2949120 | tf_op jit(solution)/shard_map/all_gather | solution.py:48
  7.3 71.8 %all-gather.10.cloned.1.call-start = ((), (), s32[]{:S(2)}) async-start(), calls=%async_computation.1 | async-start | bytes 1327104 | tf_op jit(solution)/shard_map/all_gather | solution.py:55
  8.0 114.4 %all-gather.14.cloned.1.call-start = ((), (), s32[]{:S(2)}) async-start(), calls=%async_computation.3 | async-start | bytes 1327104 | tf_op jit(solution)/shard_map/all_gather | solution.py:56
  8.7 168.2 %all-gather.12.cloned.1.call-start = ((), (), s32[]{:S(2)}) async-start(), calls=%async_computation.2 | async-start | bytes 2654208 | tf_op jit(solution)/shard_map/all_gather | solution.py:54
  9.3 220.6 %all-gather.16.cloned.1.call-start = ((), (), s32[]{:S(2)}) async-start(), calls=%async_computation.4 | async-start | bytes 2654208 | tf_op jit(solution)/shard_map/all_gather | solution.py:123
  9.9 278.3 %all-reduce.3.cloned.1.call-start = ((), (), s32[]{:S(2)}) async-start(), calls=%async_computation.5 | async-start | bytes 4718592 | tf_op jit(solution)/shard_map/psum | solution.py:126
  37.5 41.5 %copy-start = (bf16[256,4608]{1,0:T(8,128)(2,1)S(1)}, bf16[256,4608]{1,0:T(8,128)(2,1)}, u32[]{:S(2)}) copy-start(bf16[256,4608]{1,0:T(8,128)(2,1)} %all-gather.8.cloned.1.call-done) | copy-start | bytes 7077892
  229.9 60.7 %copy-start.3 = (f32[4608]{0:T(1024)S(1)}, f32[4608]{0:T(1024)}, u32[]{:S(2)}) copy-start(f32[4608]{0:T(1024)} %param.15) | copy-start | bytes 55300
  233.9 56.8 %copy-start.1 = (bf16[256,4608]{1,0:T(8,128)(2,1)S(1)}, bf16[256,4608]{1,0:T(8,128)(2,1)}, u32[]{:S(2)}) copy-start(bf16[256,4608]{1,0:T(8,128)(2,1)} %all-gather.8.cloned.1.call-done) | copy-start | bytes 7077892
  288.2 2.4 copy-start.2
Sparse Core Ops, SparseCore 0:
  8.9 26.7 all-gather.7
  37.9 41.1 all-gather.9
  81.2 41.1 all-gather.13
  124.5 52.4 all-gather.11
  179.0 50.8 all-gather.15
  234.0 54.1 all-reduce.2
where the time goes:
time: 300 us
  waiting for transfers between devices  168 us (56%)
  blocking collectives  89.8 us (30%)
  matrix products  16.3 us (5%)
  between operations  14.3 us (5%)
  other arithmetic  9.87 us (3%)
    psum x1, waiting for transfers between devices, local(): lax.psum(partial_proj.astype(jnp.bfloat16), 'head').astype(jnp.float32)  54.4 us
    all_gather x1, waiting for transfers between devices, local(): lax.all_gather(w_out, 'seq', axis=1, tiled=True)  44.5 us
    all_gather x1, waiting for transfers between devices, local(): lax.all_gather(w_key, 'seq', axis=0, tiled=True)  39.1 us
    all_gather x1, blocking collectives, local(): keys_all = lax.all_gather(rk, 'seq', axis=0, tiled=True)  34.4 us
    all_gather x1, blocking collectives, local(): values_all = lax.all_gather(vb, 'seq', axis=0, tiled=True)  32.3 us
    unnamed x1, blocking collectives  23.1 us
    all_gather x1, waiting for transfers between devices, local(): lax.all_gather(w_query, 'seq', axis=0, tiled=True)  20 us
    dot_general x3, matrix products, local(): jnp.dot(normed, piece, preferred_element_type=jnp.float32)  7.5 us
  transfers between devices with their start and end apart: 6, of which 5 were waited for; matrix products, arithmetic and copies ran while one was open for 6% of the time, Pallas kernels for 0%

commit v1 on v0

--- a/solution.py
+++ b/solution.py
@@ -82,8 +82,11 @@
         jnp.zeros((kv_count, GROUP * rows, HD), jnp.float32),
         jnp.zeros((kv_count, GROUP * rows), jnp.float32),
     )
-    keys_all = lax.all_gather(rk, "seq", axis=0, tiled=True)
-    values_all = lax.all_gather(vb, "seq", axis=0, tiled=True)
+    keys_all, values_all = jnp.split(
+        lax.all_gather(jnp.concatenate([rk, vb], axis=1), "seq", axis=0, tiled=True),
+        [rk.shape[1]],
+        axis=1,
+    )
     count = keys_all.shape[0]
     block = 1024
     steps_total = count // block

time: 300 us -> 337 us (1.12)
  waiting for transfers between devices: 168 us -> 270 us
  blocking collectives: 89.8 us -> 23.1 us
    all_gather x2 -> x0, blocking collectives: 66.7 us -> none  [the longest x1 34.4 us: local(): keys_all = lax.all_gather(rk, 'seq', axis=0, tiled=True)]
    all_gather x0 -> x1, waiting for transfers between devices: none -> 36.7 us  [local(): lax.all_gather(jnp.concatenate([rk, vb], axis=1), 'seq', axis=0, tiled=True)]
    all_gather x1, waiting for transfers between devices: 6.33 us -> 39.4 us  [local(): lax.all_gather(w_value, 'seq', axis=0, tiled=True)]
    all_gather x1, waiting for transfers between devices: 20 us -> 48.6 us  [local(): lax.all_gather(w_query, 'seq', axis=0, tiled=True)]
    all_gather x1, waiting for transfers between devices: 44.5 us -> 48.2 us  [local(): lax.all_gather(w_out, 'seq', axis=1, tiled=True)]
  transfers between devices with their start and end apart: 6 -> 7, of which waited for: 5 -> 6; matrix products, arithmetic and copies ran while one was open for 6% -> 6% of each run, Pallas kernels for 0% -> 0%
where the time goes in v1:
time: 337 us
  waiting for transfers between devices  270 us (80%)
  blocking collectives  23.1 us (7%)
  matrix products  14.4 us (4%)
  between operations  14.3 us (4%)
  other arithmetic  10.5 us (3%)
    psum x1, waiting for transfers between devices, local(): lax.psum(partial_proj.astype(jnp.bfloat16), 'head').astype(jnp.float32)  54.3 us
    all_gather x1, waiting for transfers between devices, local(): lax.all_gather(w_query, 'seq', axis=0, tiled=True)  48.6 us
    all_gather x1, waiting for transfers between devices, local(): lax.all_gather(w_out, 'seq', axis=1, tiled=True)  48.2 us
    all_gather x1, waiting for transfers between devices, local(): lax.all_gather(w_key, 'seq', axis=0, tiled=True)  40.1 us
    all_gather x1, waiting for transfers between devices, local(): lax.all_gather(w_value, 'seq', axis=0, tiled=True)  39.4 us
    all_gather x1, waiting for transfers between devices, local(): lax.all_gather(jnp.concatenate([rk, vb], axis=1), 'seq', axis=0, tiled=True)  36.7 us
    unnamed x1, blocking collectives  23.1 us
    dot_general x3, matrix products, local(): jnp.dot(normed, piece, preferred_element_type=jnp.float32)  7.56 us
  transfers between devices with their start and end apart: 7, of which 6 were waited for; matrix products, arithmetic and copies ran while one was open for 6% of the time, Pallas kernels for 0%

profile of v1, /device:TPU:0, one launch (start us, length us, event | category | flops | bytes accessed | tf_op | source)
XLA Modules:
  0.0 336.5 jit_solution(11181062297098965598)
XLA Ops:
  6.5 0.7 all-gather.8.cloned.1.call-update
  7.3 0.7 all-gather.10.cloned.1.call-update
  8.1 0.7 all-gather.12.cloned.1.call-update
  9.4 1.2 dynamic-slice
  11.3 0.8 convert_reduce_fusion
  12.3 23.1 %all-reduce = f32[64]{0:T(128)S(1)} all-reduce(f32[64]{0:T(128)S(1)} %dynamic-update-slice), channel_id=2, replica_groups=mesh['seq'=8,'head'=4] {'seq'}, use_global_device_ids=true, to_apply=%add | all-reduce | flops 64 | bytes 512
  35.8 0.8 select_reduce_fusion
  36.6 2.4 fusion.14
  39.0 40.1 %all-gather.10.cloned.1.call-done = bf16[4608,128]{1,0:T(8,128)(2,1)} async-done(((bf16[576,128]{1,0:T(8,128)(2,1)}), bf16[4608,128]{1,0:T(8,128)(2,1)}) %all-gather.10.cloned.1.call-update) | async-done | bytes 1179664 | tf_op jit(solution)/shard_map/all_gather | solution.py:55
  79.0 2.3 convolution_bitcast_fusion.1
  81.7 39.4 %all-gather.12.cloned.1.call-done = bf16[4608,128]{1,0:T(8,128)(2,1)} async-done(((bf16[576,128]{1,0:T(8,128)(2,1)}), bf16[4608,128]{1,0:T(8,128)(2,1)}) %all-gather.12.cloned.1.call-update) | async-done | bytes 1179664 | tf_op jit(solution)/shard_map/all_gather | solution.py:56
  121.1 2.3 convolution_convert_fusion.1
  125.1 48.6 %all-gather.16.cloned.1.call-done = bf16[4608,256]{1,0:T(8,128)(2,1)} async-done(((bf16[576,256]{1,0:T(8,128)(2,1)}), bf16[4608,256]{1,0:T(8,128)(2,1)}) %all-gather.16.cloned.1.call-update) | async-done | bytes 2359312 | tf_op jit(solution)/shard_map/all_gather | solution.py:54
  173.6 2.9 fusion.29
  176.8 36.7 %all-gather.14.cloned.1.call-done = bf16[2048,256]{0,1:T(8,128)(2,1)} async-done(((bf16[256,256]{0,1:T(8,128)(2,1)}), bf16[2048,256]{0,1:T(8,128)(2,1)}) %all-gather.14.cloned.1.call-update) | async-done | bytes 1048592 | tf_op jit(solution)/shard_map/all_gather | solution.py:86
  213.5 1.3 fusion.34
  214.8 3.1 while.31
  214.9 1.0 fusion.48
  216.4 1.0 fusion.48
  218.2 48.2 %all-gather.18.cloned.1.call-done = bf16[256,4608]{0,1:T(8,128)(2,1)} async-done(((bf16[256,576]{0,1:T(8,128)(2,1)}), bf16[256,4608]{0,1:T(8,128)(2,1)}) %all-gather.18.cloned.1.call-update) | async-done | bytes 2359312 | tf_op jit(solution)/shard_map/all_gather | solution.py:126
  266.4 3.9 %convolution_convert_fusion = bf16[256,4608]{1,0:T(8,128)(2,1)} fusion(bf16[256,256]{0,1:T(8,128)(2,1)S(1)} %bitcast.60, bf16[256,4608]{0,1:T(8,128)(2,1)} %all-gather.18.cloned.1.call-done), kind=kOutput, calls=%fused_computation.21 | convolution fusion | flops 605159424 | bytes 4849664 | tf_op jit(solution)/shard_map/dot_general | solution.py:125
  270.4 54.3 %all-reduce.3.cloned.1.call-done = bf16[256,4608]{1,0:T(8,128)(2,1)} async-done(((bf16[256,4608]{1,0:T(8,128)(2,1)}), bf16[256,4608]{1,0:T(8,128)(2,1)}) %all-reduce.3.cloned.1.call-update) | async-done | bytes 2359312 | tf_op jit(solution)/shard_map/psum | solution.py:129
  324.7 2.4 fusion.12
  327.1 2.6 fusion.17
  (63 shorter events, 4.9 us)
Async XLA Ops:
  6.5 72.5 %copy-start.4 = (f32[4608]{0:T(1024)S(1)}, f32[4608]{0:T(1024)}, u32[]{:S(2)}) copy-start(f32[4608]{0:T(1024)} %param.14) | copy-start | bytes 55300
  6.5 30.0 %all-gather.8.cloned.1.call-start = ((), (), s32[]{:S(2)}) async-start(), calls=%async_computation | async-start | bytes 2949120 | tf_op jit(solution)/shard_map/all_gather | solution.py:48
  7.3 71.8 %all-gather.10.cloned.1.call-start = ((), (), s32[]{:S(2)}) async-start(), calls=%async_computation.1 | async-start | bytes 1327104 | tf_op jit(solution)/shard_map/all_gather | solution.py:55
  8.0 113.1 %all-gather.12.cloned.1.call-start = ((), (), s32[]{:S(2)}) async-start(), calls=%async_computation.2 | async-start | bytes 1327104 | tf_op jit(solution)/shard_map/all_gather | solution.py:56
  8.7 164.9 %all-gather.16.cloned.1.call-start = ((), (), s32[]{:S(2)}) async-start(), calls=%async_computation.4 | async-start | bytes 2654208 | tf_op jit(solution)/shard_map/all_gather | solution.py:54
  9.3 204.2 %all-gather.14.cloned.1.call-start = ((), (), s32[]{:S(2)}) async-start(), calls=%async_computation.3 | async-start | bytes 1179648 | tf_op jit(solution)/shard_map/all_gather | solution.py:86
  36.6 42.4 %copy-start = (bf16[256,4608]{1,0:T(8,128)(2,1)S(1)}, bf16[256,4608]{1,0:T(8,128)(2,1)}, u32[]{:S(2)}) copy-start(bf16[256,4608]{1,0:T(8,128)(2,1)} %all-gather.8.cloned.1.call-done) | copy-start | bytes 7077892
  124.1 142.3 %all-gather.18.cloned.1.call-start = ((), (), s32[]{:S(2)}) async-start(), calls=%async_computation.5 | async-start | bytes 2654208 | tf_op jit(solution)/shard_map/all_gather | solution.py:126
  124.7 200.0 %all-reduce.3.cloned.1.call-start = ((), (), s32[]{:S(2)}) async-start(), calls=%async_computation.6 | async-start | bytes 4718592 | tf_op jit(solution)/shard_map/psum | solution.py:129
  266.4 60.7 %copy-start.3 = (f32[4608]{0:T(1024)S(1)}, f32[4608]{0:T(1024)}, u32[]{:S(2)}) copy-start(f32[4608]{0:T(1024)} %param.15) | copy-start | bytes 55300
  270.3 56.8 %copy-start.1 = (bf16[256,4608]{1,0:T(8,128)(2,1)S(1)}, bf16[256,4608]{1,0:T(8,128)(2,1)}, u32[]{:S(2)}) copy-start(bf16[256,4608]{1,0:T(8,128)(2,1)} %all-gather.8.cloned.1.call-done) | copy-start | bytes 7077892
  324.7 2.4 copy-start.2
Sparse Core Ops, SparseCore 0:
  8.9 26.7 all-gather.7
  37.9 41.1 all-gather.9
  81.2 39.8 all-gather.11
  123.1 50.4 all-gather.15
  175.5 37.9 all-gather.13
  215.5 50.8 all-gather.17
  270.5 54.1 all-reduce.2
